TPU v7x, 32 devices: a whole 2x2x4 slice. The times are simulated.
32 devices in a mesh: step: 2 (over y), seq: 16 (over z, x, core).
Axes of the slice: x: 2, y: 2, z: 4, core: 2. Of those that a mesh axis runs over, the one named last changes fastest.
Arguments:
- token_ids: int32 [1536], P('seq'), may hold values from 0 to 64127
- positions: int32 [1536], P('seq'), may hold values from 0 to 511, as said below
- embed_table: bfloat16 [64128, 4096], P('seq', 'step'), may hold values from -6 to 6
- norm_gain: float32 [4096], replicated, may hold values from 0.25 to 1.75
- query_weight: bfloat16 [4096, 4096], P('seq', 'step'), may hold values from -1 to 1
- key_weight: bfloat16 [4096, 1024], P('seq', 'step'), may hold values from -5 to 5
- value_weight: bfloat16 [4096, 1024], P('seq', 'step'), may hold values from -0.09375 to 0.09375
- path_points: float32 [2], replicated, may hold values from 0 to 1
- probe_direction: bfloat16 [1536, 4096], P('seq', 'step'), may hold values from -6 to 6
Outputs:
- attributions: float32 [1536, 4096], P('seq', 'step')
Inputs may be any that keep to these rules, and one draw needn't show every extreme that they name: positions[0] is 0 and each later entry is 0 or one more than the entry before; at least one document has exactly 512 tokens.
All inputs are finite; a program needn't handle non-finite values.
Results may differ from a plain program's by a relative error of at most 0.006.
The roundings to bfloat16 on the way count: a program that leaves them out, or rounds other values in their place, can miss the bound.
Values may be sent and summed in bfloat16 or wider, within the bound.
A program may use at most 128 MiB of HBM per device.

v0:
```python
import math

import jax
import jax.numpy as jnp
from jax import lax
from jax.sharding import PartitionSpec as P

HEAD = 128
REACH = 6


NORM_EPSILON = 1e-05
ROPE_BASE = 500000.0
MASKED = -1e30


def passed_along(array, axis, by):
    size = lax.axis_size(axis)
    pairs = [(i, i + by) for i in range(size) if 0 <= i + by < size]
    return lax.ppermute(array, axis, pairs)


def rope_tables(positions, head_size):
    halfway = head_size // 2
    frequency = ROPE_BASE ** (-2.0 * jnp.arange(halfway, dtype=jnp.float32) / head_size)
    angles = positions.astype(jnp.float32)[:, None] * frequency[None, :]
    return (jnp.cos(angles), jnp.sin(angles))


def rotate(vectors, cosine, sinusoid):
    halfway = vectors.shape[-1] // 2
    former = vectors[..., :halfway]
    latter = vectors[..., halfway:]
    cos_rows = cosine[:, None, :]
    sin_rows = sinusoid[:, None, :]
    return jnp.concatenate(
        [former * cos_rows - latter * sin_rows, latter * cos_rows + former * sin_rows], axis=-1
    )


def unrotate(gradient, cosine, sinusoid):
    halfway = gradient.shape[-1] // 2
    former = gradient[..., :halfway]
    latter = gradient[..., halfway:]
    cos_rows = cosine[:, None, :]
    sin_rows = sinusoid[:, None, :]
    return jnp.concatenate(
        [former * cos_rows + latter * sin_rows, latter * cos_rows - former * sin_rows], axis=-1
    )


def per_device(
    token_ids,
    positions,
    embed_table,
    norm_gain,
    query_weight,
    key_weight,
    value_weight,
    path_points,
    probe_direction,
):
    seq_len = token_ids.shape[0]
    step_count = path_points.shape[0]
    head_size = HEAD
    query_heads = query_weight.shape[1] // head_size
    shared_heads = key_weight.shape[1] // head_size
    group_size = query_heads // shared_heads
    query_cols = query_heads * head_size
    shared_cols = shared_heads * head_size
    score_scale = 1.0 / math.sqrt(head_size)
    seq_index = lax.axis_index("seq")
    seq_count = lax.axis_size("seq")
    all_rows = step_count * seq_len
    ids_all = lax.all_gather(token_ids, "seq", axis=0, tiled=True)
    wanted = jnp.concatenate(
        [ids_all.reshape(seq_count, seq_len), jnp.zeros((seq_count, 1), jnp.int32)], axis=1
    ).reshape(seq_count * (seq_len + 1))
    shard_rows = embed_table.shape[0]
    first_row = seq_index * shard_rows
    local = wanted - first_row
    owned = (local >= 0) & (local < shard_rows)
    picked = jnp.take(embed_table, jnp.clip(local, 0, shard_rows - 1), axis=0)
    own_columns = lax.psum_scatter(
        jnp.where(owned[:, None], picked.astype(jnp.float32), 0.0),
        "seq",
        scatter_dimension=0,
        tiled=True,
    )
    looked = lax.all_gather(own_columns.astype(jnp.bfloat16), "step", axis=1, tiled=True).astype(
        jnp.float32
    )
    features = looked.shape[1]
    embedded = looked[:seq_len]
    baseline = looked[seq_len:]
    difference = embedded - baseline
    inputs = baseline[None] + path_points[:, None, None] * difference[None]
    radius = jnp.sqrt(jnp.mean(inputs * inputs, axis=-1, keepdims=True) + NORM_EPSILON)
    unitized = inputs / radius
    normed = (unitized * norm_gain).astype(jnp.bfloat16).reshape(all_rows, features)
    joined = jnp.concatenate([query_weight, key_weight, value_weight], axis=1)
    joined_cols = joined.shape[1]
    projected = jnp.dot(
        normed,
        lax.all_gather(joined, "seq", axis=0, tiled=True),
        preferred_element_type=jnp.float32,
    )
    projected = projected.reshape(step_count, seq_len, joined_cols)
    cosine, sinusoid = rope_tables(positions, head_size)
    queries = rotate(
        projected[..., :query_cols].reshape(step_count, seq_len, query_heads, head_size),
        cosine,
        sinusoid,
    ).astype(jnp.bfloat16)
    key_rows = rotate(
        projected[..., query_cols : query_cols + shared_cols].reshape(
            step_count, seq_len, shared_heads, head_size
        ),
        cosine,
        sinusoid,
    ).astype(jnp.bfloat16)
    key_rows = key_rows.reshape(step_count, seq_len, shared_cols)
    value_rows = projected[..., query_cols + shared_cols :].astype(jnp.bfloat16)
    blocks = [(key_rows, value_rows)]
    current = (key_rows, value_rows)
    for distance in range(REACH):
        current = passed_along((current[0], current[1]), "seq", 1)
        blocks.append(current)
    ordered = blocks[::-1]
    key_all = jnp.concatenate([member[0] for member in ordered], axis=1)
    value_all = jnp.concatenate([member[1] for member in ordered], axis=1)
    reach_keys = key_all.shape[1]
    key_all = key_all.reshape(step_count, reach_keys, shared_heads, head_size)
    value_all = value_all.reshape(step_count, reach_keys, shared_heads, head_size)
    query_pos = seq_index * seq_len + jnp.arange(seq_len, dtype=jnp.int32)
    key_pos = (seq_index - REACH) * seq_len + jnp.arange(reach_keys, dtype=jnp.int32)
    visible = (key_pos[None, :] <= query_pos[:, None]) & (
        key_pos[None, :] >= (query_pos - positions)[:, None]
    )
    query_split = queries.reshape(step_count, seq_len, shared_heads, group_size, head_size)
    probe_split = probe_direction.reshape(seq_len, shared_heads, group_size, head_size)
    scores = (
        jnp.einsum("sqgae,skge->sgaqk", query_split, key_all, preferred_element_type=jnp.float32)
        * score_scale
    )
    scores = jnp.where(visible, scores, MASKED)
    row_max = jnp.max(scores, axis=-1, keepdims=True)
    powers = jnp.exp(scores - row_max)
    attention = powers / jnp.sum(powers, axis=-1, keepdims=True)
    attention_bf = attention.astype(jnp.bfloat16)
    attention_grad = jnp.einsum(
        "qgae,skge->sgaqk", probe_split, value_all, preferred_element_type=jnp.float32
    )
    row_dot = jnp.sum(attention * attention_grad, axis=-1, keepdims=True)
    score_grad = (attention * (attention_grad - row_dot) * score_scale).astype(jnp.bfloat16)
    query_grad = jnp.einsum(
        "sgaqk,skge->sqgae", score_grad, key_all, preferred_element_type=jnp.float32
    )
    query_grad = query_grad.reshape(step_count, seq_len, query_heads, head_size)
    key_grad = jnp.einsum(
        "sgaqk,sqgae->skge", score_grad, query_split, preferred_element_type=jnp.float32
    ).reshape(step_count, reach_keys, shared_cols)
    value_grad = jnp.einsum(
        "sgaqk,qgae->skge", attention_bf, probe_split, preferred_element_type=jnp.float32
    ).reshape(step_count, reach_keys, shared_cols)
    pieces = [
        (
            key_grad[:, which * seq_len : (which + 1) * seq_len],
            value_grad[:, which * seq_len : (which + 1) * seq_len],
        )
        for which in range(REACH + 1)
    ]
    carried = pieces[0]
    for which in range(1, REACH + 1):
        arrived = passed_along(carried, "seq", -1)
        carried = (arrived[0] + pieces[which][0], arrived[1] + pieces[which][1])
    key_total, value_total = carried
    query_back = (
        unrotate(query_grad, cosine, sinusoid).astype(jnp.bfloat16).reshape(all_rows, query_cols)
    )
    key_back = (
        unrotate(key_total.reshape(step_count, seq_len, shared_heads, head_size), cosine, sinusoid)
        .astype(jnp.bfloat16)
        .reshape(all_rows, shared_cols)
    )
    value_back = value_total.astype(jnp.bfloat16).reshape(all_rows, shared_cols)
    joined_grad = jnp.concatenate([query_back, key_back, value_back], axis=1)
    contract = (((1,), (1,)), ((), ()))
    norm_grad = lax.dot_general(
        joined_grad,
        lax.all_gather(joined, "seq", axis=0, tiled=True),
        contract,
        preferred_element_type=jnp.float32,
    )
    scaled = norm_gain * norm_grad.reshape(step_count, seq_len, features)
    input_grad = (scaled - unitized * jnp.mean(scaled * unitized, axis=-1, keepdims=True)) / radius
    partial_value = difference * jnp.sum(input_grad, axis=0) / step_count
    return lax.psum_scatter(partial_value, "step", scatter_dimension=1, tiled=True)


def solution(mesh):
    in_specs = (
        P("seq"),
        P("seq"),
        P("seq", "step"),
        P(),
        P("seq", "step"),
        P("seq", "step"),
        P("seq", "step"),
        P(),
        P("seq", "step"),
    )
    out_specs = P("seq", "step")
    return jax.shard_map(
        per_device, mesh=mesh, in_specs=in_specs, out_specs=out_specs, check_vma=False
    )
```

profile of v0, /device:TPU:0, one launch (start us, length us, event | category | flops | bytes accessed | tf_op | source)
XLA Modules:
  0.0 590.1 jit_solution(958622772062197762)
XLA Ops:
  6.5 2.7 pad_maximum_fusion
  10.9 14.3 %all-reduce.1 = s32[1536]{0:T(1024)S(1)} all-reduce(s32[1536]{0:T(1024)S(1)} %dynamic-update-slice), channel_id=1, replica_groups=mesh['step'=2,'seq'=16] {'seq'}, use_global_device_ids=true, to_apply=%add.1 | all-reduce | flops 1536 | bytes 12288
  25.6 22.4 %gather_fusion = bf16[1552,2048]{1,0:T(8,128)(2,1)} fusion(bf16[4008,2048]{1,0:T(8,128)(2,1)} %param.11, s32[2048]{0:T(1024)S(1)} %pad_clamp_fusion), kind=kCustom, calls=%fused_computation | custom fusion | bytes 12720192 | tf_op jit(solution)/shard_map/jit(_take)/gather | solution.py:83
  48.1 8.7 %convert_select_fusion = f32[1552,2048]{1,0:T(8,128)} fusion(bf16[1552,2048]{1,0:T(8,128)(2,1)} %gather_fusion, pred[1552]{0:T(1024)(128)(4,1)S(1)} %compare_and_fusion.1, pred[1552]{0:T(1024)(128)(4,1)S(1)} %and.22), kind=kLoop, calls=%fused_computation.5 | loop fusion | flops 9535488 | bytes 19074080 | tf_op jit(solution)/shard_map/jit(_where)/select_n | solution.py:85
  56.7 217.8 %fusion = f32[104,2048]{1,0:T(8,128)S(1)} fusion(f32[1552,2048]{1,0:T(8,128)} %convert_select_fusion), kind=kCustom, calls=%all-reduce-scatter | all-reduce-scatter fusion | flops 3407873 | bytes 13566464
  274.5 13.5 %collective-permute-start.25 = (bf16[1,2048]{1,0:T(2,128)(2,1)S(1)}, bf16[1,2048]{1,0:T(2,128)(2,1)S(1)}, u32[]{:S(2)}, u32[]{:S(2)}) collective-permute-start(bf16[1,2048]{1,0:T(2,128)(2,1)S(1)} %slice.138), channel_id=1, source_target_pairs={{0,2},{1,3},{2,4},{3,5},{4,6},{5,7},{6,8},{7,9},{8,10},{9,11},{10,... | collective-permute-start | bytes 12296
  292.8 10.7 %all_gather.11 = bf16[97,4096]{1,0:T(8,128)(2,1)S(1)} all-gather(bf16[97,2048]{1,0:T(8,128)(2,1)S(1)} %dynamic-slice_convert_fusion), channel_id=1, replica_groups=mesh['step'=2,'seq'=16] {'step'}, dimensions={1}, use_global_device_ids=true | all-gather | bytes 1191936 | tf_op jit(solution)/shard_map/all_gather | solution.py:90
  304.8 10.8 %fusion.3 = f32[2,96,3072]{2,1,0:T(8,128)S(1)} fusion(bf16[4096,3072]{1,0:T(8,128)(2,1)} %all-gather.2.cloned.1.call-done, f32[2,96]{1,0:T(2,128)S(1)} %add_sqrt_fusion, f32[96,4096]{1,0:T(8,128)S(1)} %slice_subtract_fusion, f32[2]{0:T(128)S(1)} %copy-done.24, f32[4096]{0:T(1024)S(1)} %bitcast.167, f32[4096]{0:T(1024)S(1)} %copy-done.20), kind=kOutput, calls=%fused_computation.3 | convolution fusion | flops 4835770368 | bytes 29131528 | tf_op jit(solution)/shard_map/dot_general | solution.py:103
  317.9 1.9 reshape.232
  322.3 4.4 collective-permute-start
  326.8 3.6 collective-permute-start.6
  330.4 2.5 collective-permute-start.1
  333.6 5.1 collective-permute-start.7
  338.7 2.1 collective-permute-start.2
  340.8 4.2 collective-permute-start.8
  345.0 2.9 collective-permute-start.3
  347.9 2.0 reshape.235
  349.9 3.8 collective-permute-start.9
  353.7 1.9 collective-permute-start.4
  357.4 3.0 collective-permute-start.10
  360.4 2.2 collective-permute-start.5
  365.5 3.4 collective-permute-start.11
  370.4 1.6 bitcast_dynamic-update-slice_fusion.3
  372.1 1.7 bitcast_dynamic-update-slice_fusion.2
  378.1 1.6 constant_dynamic-update-slice_fusion.4
  379.7 1.6 constant_dynamic-update-slice_fusion.3
  382.7 3.7 reshape.234
  386.4 3.3 fusion.32
  389.6 6.5 %fusion.61 = (f32[2,4,4,96]{3,2,1,0:T(4,128)S(1)}, f32[2,4,4,96,672]{4,3,2,1,0:T(8,128)}) fusion(f32[2,4,672,96,4]{2,3,4,1,0:T(8,128)S(1)} %fusion.32, pred[96,672]{1,0:T(8,128)(4,1)S(1)} %copy-done.19), kind=kOutput, calls=%fused_computation.133 | output fusion | flops 12386975 | bytes 16591872 | tf_op jit(solution)/shard_map/sub | solution.py:148
  396.1 5.0 fusion.29
  401.2 33.2 %fusion.20 = f32[2,4,84,8,128]{4,3,2,1,0:T(8,128)} fusion(f32[4,2,672,96,4]{2,3,4,0,1:T(8,128)} %fusion.29, bf16[2,96,4,4,64]{4,1,3,2,0:T(8,128)(2,1)} %bitcast.157, bf16[2,96,4,4,64]{4,1,3,2,0:T(8,128)(2,1)} %bitcast.159, f32[2,4,4,96,672]{4,3,2,1,0:T(8,128)} %get-tuple-element.26, f32[2,4,4,96]{3,2,1,0:T(4,128)S(1)} %get-tuple-element.25), kind=kOutput, calls=%fused_computation.34 | convolution fusion | flops 544509568 | bytes 20066304 | tf_op jit(solution)/shard_map/sgaqk,sqgae->skge/dot_general | solution.py:160
  434.4 2.2 copy.131
  438.1 5.1 fusion.21
  452.2 2.3 fusion.18
  454.5 3.5 collective-permute-done.19
  458.0 1.9 slice_add_fusion.4
  462.2 2.0 slice_add_fusion.9
  465.5 24.8 %fusion.16 = f32[2,4,128,4,96]{2,4,3,1,0:T(8,128)} fusion(f32[4,2,672,96,4]{2,3,4,0,1:T(8,128)} %fusion.29, bf16[2,672,4,128]{3,1,2,0:T(8,128)(2,1)} %constant_dynamic-update-slice_fusion, f32[2,4,4,96,672]{4,3,2,1,0:T(8,128)} %get-tuple-element.26, f32[2,4,4,96]{3,2,1,0:T(4,128)S(1)} %get-tuple-element.25), kind=kOutput, calls=%fused_computation.22 | convolution fusion | flops 542936704 | bytes 19476480 | tf_op jit(solution)/shard_map/sgaqk,skge->sqgae/dot_general | solution.py:156
  495.9 5.3 collective-permute-done.21
  506.7 1.9 add_convert_fusion
  511.4 1.8 slice_add_fusion.1
  515.6 1.8 slice_add_fusion.6
  517.4 1.9 reshape.238
  521.1 2.0 collective-permute-done.23
  523.1 1.8 fusion.40
  525.0 15.1 %multiply_reduce_fusion = (f32[192]{0:T(256)S(1)}, f32[192,4096]{1,0:T(8,128)}) fusion(f32[192,4096]{1,0:T(8,128)} %fusion.18, f32[4096]{0:T(1024)S(1)} %copy-done.20, bf16[4096,3072]{1,0:T(8,128)(2,1)} %all-gather.2.cloned.1.call-done, bf16[192,512]{1,0:T(8,128)(2,1)} %bitcast.172, bf16[192,512]{1,0:T(8,128)(2,1)S(1)} %bitcast.171, ...), kind=kOutput, calls=%fused_computation.27 | convolution fusion | flops 4837736448 | bytes 32654080 | tf_op jit(solution)/shard_map/dot_general | solution.py:189
  540.2 3.0 divide_reduce_fusion
  544.6 38.2 %reduce-scatter.4.cloned.1.call-done = f32[96,2048]{1,0:T(8,128)} async-done(((f32[96,4096]{1,0:T(8,128)}), f32[96,2048]{1,0:T(8,128)}) %reduce-scatter.4.cloned.1.call-update) | async-done | bytes 786448 | tf_op jit(solution)/shard_map/reduce_scatter | solution.py:198
  (172 shorter events, 57.3 us)
Async XLA Ops:
  6.5 298.3 %all-gather.2.cloned.1.call-start = ((), (), s32[]{:S(2)}) async-start(), calls=%async_computation.1 | async-start | bytes 26738688 | tf_op jit(solution)/shard_map/all_gather | solution.py:105
  9.3 573.5 %reduce-scatter.4.cloned.1.call-start = ((), (), s32[]{:S(2)}) async-start(), calls=%async_computation.2 | async-start | bytes 2359296 | tf_op jit(solution)/shard_map/reduce_scatter | solution.py:198
  56.7 232.7 %copy-start.28 = (s32[96]{0:T(128)S(1)}, s32[96]{0:T(128)}, u32[]{:S(2)}) copy-start(s32[96]{0:T(128)} %param.10) | copy-start | bytes 1156
  274.5 17.1 %collective-permute-start.25 = (bf16[1,2048]{1,0:T(2,128)(2,1)S(1)}, bf16[1,2048]{1,0:T(2,128)(2,1)S(1)}, u32[]{:S(2)}, u32[]{:S(2)}) collective-permute-start(bf16[1,2048]{1,0:T(2,128)(2,1)S(1)} %slice.138), channel_id=1, source_target_pairs={{0,2},{1,3},{2,4},{3,5},{4,6},{5,7},{6,8},{7,9},{8,10},{9,11},{10,... | collective-permute-start | bytes 12296
  288.1 3.5 collective-permute-start.24
  304.8 10.9 %copy-start.21 = (f32[2,96]{1,0:T(2,128)}, f32[2,96]{1,0:T(2,128)S(1)}, u32[]{:S(2)}) copy-start(f32[2,96]{1,0:T(2,128)S(1)} %add_sqrt_fusion) | copy-start | bytes 2308
  319.8 7.0 %copy-start.4 = (f32[2,96,3072]{2,1,0:T(8,128)S(1)}, f32[2,96,3072]{2,1,0:T(8,128)}, u32[]{:S(2)}) copy-start(f32[2,96,3072]{2,1,0:T(8,128)} %copy-done.3) | copy-start | bytes 7077892
  322.3 8.0 %collective-permute-start = (bf16[2,96,512]{2,1,0:T(8,128)(2,1)S(1)}, bf16[2,96,512]{2,1,0:T(8,128)(2,1)S(1)}, u32[]{:S(2)}, u32[]{:S(2)}) collective-permute-start(bf16[2,96,512]{2,1,0:T(8,128)(2,1)S(1)} %copy_bitcast_fusion.4), channel_id=1, source_target_pairs={{0,1},{1,2},{2,3},{3,4},{4,5},{5,6},{6,7},{7,8},{8,9},{9,10},{10,1... | collective-permute-start | bytes 589832 | tf_op jit(solution)/shard_map/ppermute | solution.py:20
  326.8 6.1 %collective-permute-start.6 = (bf16[2,96,512]{2,1,0:T(8,128)(2,1)S(1)}, bf16[2,96,512]{2,1,0:T(8,128)(2,1)S(1)}, u32[]{:S(2)}, u32[]{:S(2)}) collective-permute-start(bf16[2,96,512]{2,1,0:T(8,128)(2,1)S(1)} %slice.159), channel_id=1, source_target_pairs={{0,1},{1,2},{2,3},{3,4},{4,5},{5,6},{6,7},{7,8},{8,9},{9,10},{10,1... | collective-permute-start | bytes 589832 | tf_op jit(solution)/shard_map/ppermute | solution.py:20
  330.4 10.4 %copy-start.15 = (bf16[2,96,512]{2,1,0:T(8,128)(2,1)}, bf16[2,96,512]{2,1,0:T(8,128)(2,1)S(1)}, u32[]{:S(2)}) copy-start(bf16[2,96,512]{2,1,0:T(8,128)(2,1)S(1)} %collective-permute-done) | copy-start | bytes 589828
  330.4 8.3 %collective-permute-start.1 = (bf16[2,96,512]{2,1,0:T(8,128)(2,1)S(1)}, bf16[2,96,512]{2,1,0:T(8,128)(2,1)S(1)}, u32[]{:S(2)}, u32[]{:S(2)}) collective-permute-start(bf16[2,96,512]{2,1,0:T(8,128)(2,1)S(1)} %collective-permute-done), channel_id=1, source_target_pairs={{0,1},{1,2},{2,3},{3,4},{4,5},{5,6},{6,7},{7,8},{8,9},{9,10},{10,1... | collective-permute-start | bytes 589832 | tf_op jit(solution)/shard_map/ppermute | solution.py:20
  333.6 7.2 %collective-permute-start.7 = (bf16[2,96,512]{2,1,0:T(8,128)(2,1)S(1)}, bf16[2,96,512]{2,1,0:T(8,128)(2,1)}, u32[]{:S(2)}, u32[]{:S(2)}) collective-permute-start(bf16[2,96,512]{2,1,0:T(8,128)(2,1)S(1)} %collective-permute-done.6), channel_id=1, source_target_pairs={{0,1},{1,2},{2,3},{3,4},{4,5},{5,6},{6,7},{7,8},{8,9},{9,10},{10,1... | collective-permute-start | bytes 589832 | tf_op jit(solution)/shard_map/ppermute | solution.py:20
  338.7 6.3 %copy-start.17 = (bf16[2,96,512]{2,1,0:T(8,128)(2,1)}, bf16[2,96,512]{2,1,0:T(8,128)(2,1)S(1)}, u32[]{:S(2)}) copy-start(bf16[2,96,512]{2,1,0:T(8,128)(2,1)S(1)} %collective-permute-done.1) | copy-start | bytes 589828
  338.7 6.3 %collective-permute-start.2 = (bf16[2,96,512]{2,1,0:T(8,128)(2,1)S(1)}, bf16[2,96,512]{2,1,0:T(8,128)(2,1)}, u32[]{:S(2)}, u32[]{:S(2)}) collective-permute-start(bf16[2,96,512]{2,1,0:T(8,128)(2,1)S(1)} %collective-permute-done.1), channel_id=1, source_target_pairs={{0,1},{1,2},{2,3},{3,4},{4,5},{5,6},{6,7},{7,8},{8,9},{9,10},{10,1... | collective-permute-start | bytes 589832 | tf_op jit(solution)/shard_map/ppermute | solution.py:20
  340.8 9.1 %collective-permute-start.8 = (bf16[2,96,512]{2,1,0:T(8,128)(2,1)}, bf16[2,96,512]{2,1,0:T(8,128)(2,1)}, u32[]{:S(2)}, u32[]{:S(2)}) collective-permute-start(bf16[2,96,512]{2,1,0:T(8,128)(2,1)} %collective-permute-done.7), channel_id=1, source_target_pairs={{0,1},{1,2},{2,3},{3,4},{4,5},{5,6},{6,7},{7,8},{8,9},{9,10},{10,1... | collective-permute-start | bytes 589832 | tf_op jit(solution)/shard_map/ppermute | solution.py:20
  345.0 8.7 %collective-permute-start.3 = (bf16[2,96,512]{2,1,0:T(8,128)(2,1)}, bf16[2,96,512]{2,1,0:T(8,128)(2,1)}, u32[]{:S(2)}, u32[]{:S(2)}) collective-permute-start(bf16[2,96,512]{2,1,0:T(8,128)(2,1)} %collective-permute-done.2), channel_id=1, source_target_pairs={{0,1},{1,2},{2,3},{3,4},{4,5},{5,6},{6,7},{7,8},{8,9},{9,10},{10,1... | collective-permute-start | bytes 589832 | tf_op jit(solution)/shard_map/ppermute | solution.py:20
  349.9 7.2 %slice-start = ((f32[2,96,3072]{2,1,0:T(8,128)}), f32[2,96,2048]{2,1,0:T(8,128)S(1)}, s32[]{:S(2)}) async-start(f32[2,96,3072]{2,1,0:T(8,128)} %copy-done.3), calls=%async_computation.3 | async-start | bytes 3145728 | tf_op jit(solution)/shard_map/slice | solution.py:111
  349.9 7.5 %collective-permute-start.9 = (bf16[2,96,512]{2,1,0:T(8,128)(2,1)}, bf16[2,96,512]{2,1,0:T(8,128)(2,1)S(1)}, u32[]{:S(2)}, u32[]{:S(2)}) collective-permute-start(bf16[2,96,512]{2,1,0:T(8,128)(2,1)} %collective-permute-done.8), channel_id=1, source_target_pairs={{0,1},{1,2},{2,3},{3,4},{4,5},{5,6},{6,7},{7,8},{8,9},{9,10},{10,1... | collective-permute-start | bytes 589832 | tf_op jit(solution)/shard_map/ppermute | solution.py:20
  353.7 6.7 %collective-permute-start.4 = (bf16[2,96,512]{2,1,0:T(8,128)(2,1)}, bf16[2,96,512]{2,1,0:T(8,128)(2,1)S(1)}, u32[]{:S(2)}, u32[]{:S(2)}) collective-permute-start(bf16[2,96,512]{2,1,0:T(8,128)(2,1)} %collective-permute-done.3), channel_id=1, source_target_pairs={{0,1},{1,2},{2,3},{3,4},{4,5},{5,6},{6,7},{7,8},{8,9},{9,10},{10,1... | collective-permute-start | bytes 589832 | tf_op jit(solution)/shard_map/ppermute | solution.py:20
  357.1 5.6 copy-start.11
  357.4 8.2 %collective-permute-start.10 = (bf16[2,96,512]{2,1,0:T(8,128)(2,1)S(1)}, bf16[2,96,512]{2,1,0:T(8,128)(2,1)S(1)}, u32[]{:S(2)}, u32[]{:S(2)}) collective-permute-start(bf16[2,96,512]{2,1,0:T(8,128)(2,1)S(1)} %collective-permute-done.9), channel_id=1, source_target_pairs={{0,1},{1,2},{2,3},{3,4},{4,5},{5,6},{6,7},{7,8},{8,9},{9,10},{10,1... | collective-permute-start | bytes 589832 | tf_op jit(solution)/shard_map/ppermute | solution.py:20
  360.4 8.6 %collective-permute-start.5 = (bf16[2,96,512]{2,1,0:T(8,128)(2,1)S(1)}, bf16[2,96,512]{2,1,0:T(8,128)(2,1)S(1)}, u32[]{:S(2)}, u32[]{:S(2)}) collective-permute-start(bf16[2,96,512]{2,1,0:T(8,128)(2,1)S(1)} %collective-permute-done.4), channel_id=1, source_target_pairs={{0,1},{1,2},{2,3},{3,4},{4,5},{5,6},{6,7},{7,8},{8,9},{9,10},{10,1... | collective-permute-start | bytes 589832 | tf_op jit(solution)/shard_map/ppermute | solution.py:20
  363.3 10.4 %copy-start.18 = (bf16[2,96,512]{2,1,0:T(8,128)(2,1)S(1)}, bf16[2,96,512]{2,1,0:T(8,128)(2,1)}, u32[]{:S(2)}) copy-start(bf16[2,96,512]{2,1,0:T(8,128)(2,1)} %copy-done.17) | copy-start | bytes 589828
  363.3 11.2 %copy-start.16 = (bf16[2,96,512]{2,1,0:T(8,128)(2,1)S(1)}, bf16[2,96,512]{2,1,0:T(8,128)(2,1)}, u32[]{:S(2)}) copy-start(bf16[2,96,512]{2,1,0:T(8,128)(2,1)} %copy-done.15) | copy-start | bytes 589828
  363.3 11.9 %copy-start.8 = (bf16[2,96,4,64]{3,1,2,0:T(8,128)(2,1)S(1)}, bf16[2,96,4,64]{3,1,2,0:T(8,128)(2,1)}, u32[]{:S(2)}) copy-start(bf16[2,96,4,64]{3,1,2,0:T(8,128)(2,1)} %copy-done.7) | copy-start | bytes 294916
  365.5 15.8 %copy-start.14 = (bf16[2,96,512]{2,1,0:T(8,128)(2,1)S(1)}, bf16[2,96,512]{2,1,0:T(8,128)(2,1)}, u32[]{:S(2)}) copy-start(bf16[2,96,512]{2,1,0:T(8,128)(2,1)} %copy-done.13) | copy-start | bytes 589828
  365.5 16.5 %copy-start.5 = (f32[2,96,3072]{2,1,0:T(8,128)S(1)}, f32[2,96,3072]{2,1,0:T(8,128)}, u32[]{:S(2)}) copy-start(f32[2,96,3072]{2,1,0:T(8,128)} %copy-done.3) | copy-start | bytes 7077892
  365.5 10.5 %collective-permute-start.11 = (bf16[2,96,512]{2,1,0:T(8,128)(2,1)S(1)}, bf16[2,96,512]{2,1,0:T(8,128)(2,1)S(1)}, u32[]{:S(2)}, u32[]{:S(2)}) collective-permute-start(bf16[2,96,512]{2,1,0:T(8,128)(2,1)S(1)} %collective-permute-done.10), channel_id=1, source_target_pairs={{0,1},{1,2},{2,3},{3,4},{4,5},{5,6},{6,7},{7,8},{8,9},{9,10},{10,1... | collective-permute-start | bytes 589832 | tf_op jit(solution)/shard_map/ppermute | solution.py:20
  389.6 6.5 %copy-start.6 = (bf16[2,672,4,128]{3,2,1,0:T(4,128)(2,1)S(1)}, bf16[2,672,4,128]{3,2,1,0:T(4,128)(2,1)}, u32[]{:S(2)}) copy-start(bf16[2,672,4,128]{3,2,1,0:T(4,128)(2,1)} %reshape.234) | copy-start | bytes 4128772
  389.6 6.5 %copy-start.9 = (bf16[96,4,4,128]{3,2,1,0:T(4,128)(2,1)S(1)}, bf16[96,4,4,128]{3,2,1,0:T(4,128)(2,1)}, u32[]{:S(2)}) copy-start(bf16[96,4,4,128]{3,2,1,0:T(4,128)(2,1)} %reshape.235) | copy-start | bytes 1179652
  436.6 13.3 %copy-start.1 = (f32[2,4,84,8,128]{4,3,1,2,0:T(8,128)}, f32[2,4,84,8,128]{4,3,1,2,0:T(8,128)S(1)}, u32[]{:S(2)}) copy-start(f32[2,4,84,8,128]{4,3,1,2,0:T(8,128)S(1)} %copy.131) | copy-start | bytes 8257540
  436.6 8.4 %collective-permute-start.12 = (f32[2,96,512]{2,1,0:T(8,128)S(1)}, f32[2,96,512]{2,1,0:T(8,128)S(1)}, u32[]{:S(2)}, u32[]{:S(2)}) collective-permute-start(f32[2,96,512]{2,1,0:T(8,128)S(1)} %slice.122), channel_id=1, source_target_pairs={{1,0},{2,1},{3,2},{4,3},{5,4},{6,5},{7,6},{8,7},{9,8},{10,9},{11,1... | collective-permute-start | bytes 1179656 | tf_op jit(solution)/shard_map/ppermute | solution.py:20
  443.7 8.3 %copy-start.25 = (f32[2]{0:T(128)S(1)}, f32[2]{0:T(128)}, u32[]{:S(2)}) copy-start(f32[2]{0:T(128)} %param.16) | copy-start | bytes 28
  443.7 8.5 %copy-start.22 = (f32[2,96]{1,0:T(2,128)S(1)}, f32[2,96]{1,0:T(2,128)}, u32[]{:S(2)}) copy-start(f32[2,96]{1,0:T(2,128)} %copy-done.21) | copy-start | bytes 2308
  443.7 4.0 collective-permute-start.18
  445.1 4.8 collective-permute-start.13
  448.6 9.4 %collective-permute-start.19 = (f32[2,96,512]{2,1,0:T(8,128)}, f32[2,96,512]{2,1,0:T(8,128)}, u32[]{:S(2)}, u32[]{:S(2)}) collective-permute-start(f32[2,96,512]{2,1,0:T(8,128)} %slice_add_fusion.5), channel_id=1, source_target_pairs={{1,0},{2,1},{3,2},{4,3},{5,4},{6,5},{7,6},{8,7},{9,8},{10,9},{11,1... | collective-permute-start | bytes 1179656 | tf_op jit(solution)/shard_map/ppermute | solution.py:20
  450.7 11.5 %collective-permute-start.14 = (f32[2,96,512]{2,1,0:T(8,128)}, f32[2,96,512]{2,1,0:T(8,128)}, u32[]{:S(2)}, u32[]{:S(2)}) collective-permute-start(f32[2,96,512]{2,1,0:T(8,128)} %slice_add_fusion.10), channel_id=1, source_target_pairs={{1,0},{2,1},{3,2},{4,3},{5,4},{6,5},{7,6},{8,7},{9,8},{10,9},{11,1... | collective-permute-start | bytes 1179656 | tf_op jit(solution)/shard_map/ppermute | solution.py:20
  459.9 30.4 %collective-permute-start.20 = (f32[2,96,512]{2,1,0:T(8,128)}, f32[2,96,512]{2,1,0:T(8,128)}, u32[]{:S(2)}, u32[]{:S(2)}) collective-permute-start(f32[2,96,512]{2,1,0:T(8,128)} %slice_add_fusion.4), channel_id=1, source_target_pairs={{1,0},{2,1},{3,2},{4,3},{5,4},{6,5},{7,6},{8,7},{9,8},{10,9},{11,1... | collective-permute-start | bytes 1179656 | tf_op jit(solution)/shard_map/ppermute | solution.py:20
  464.2 28.7 %collective-permute-start.15 = (f32[2,96,512]{2,1,0:T(8,128)}, f32[2,96,512]{2,1,0:T(8,128)}, u32[]{:S(2)}, u32[]{:S(2)}) collective-permute-start(f32[2,96,512]{2,1,0:T(8,128)} %slice_add_fusion.9), channel_id=1, source_target_pairs={{1,0},{2,1},{3,2},{4,3},{5,4},{6,5},{7,6},{8,7},{9,8},{10,9},{11,1... | collective-permute-start | bytes 1179656 | tf_op jit(solution)/shard_map/ppermute | solution.py:20
  491.6 9.7 %collective-permute-start.21 = (f32[2,96,512]{2,1,0:T(8,128)S(1)}, f32[2,96,512]{2,1,0:T(8,128)S(1)}, u32[]{:S(2)}, u32[]{:S(2)}) collective-permute-start(f32[2,96,512]{2,1,0:T(8,128)S(1)} %slice_add_fusion.3), channel_id=1, source_target_pairs={{1,0},{2,1},{3,2},{4,3},{5,4},{6,5},{7,6},{8,7},{9,8},{10,9},{11,1... | collective-permute-start | bytes 1179656 | tf_op jit(solution)/shard_map/ppermute | solution.py:20
  494.1 10.3 %collective-permute-start.16 = (f32[2,96,512]{2,1,0:T(8,128)S(1)}, f32[2,96,512]{2,1,0:T(8,128)S(1)}, u32[]{:S(2)}, u32[]{:S(2)}) collective-permute-start(f32[2,96,512]{2,1,0:T(8,128)S(1)} %slice_add_fusion.8), channel_id=1, source_target_pairs={{1,0},{2,1},{3,2},{4,3},{5,4},{6,5},{7,6},{8,7},{9,8},{10,9},{11,1... | collective-permute-start | bytes 1179656 | tf_op jit(solution)/shard_map/ppermute | solution.py:20
  495.4 11.4 %copy-start.12 = (f32[96,64]{1,0:T(8,128)S(1)}, f32[96,64]{1,0:T(8,128)}, u32[]{:S(2)}) copy-start(f32[96,64]{1,0:T(8,128)} %get-tuple-element.20) | copy-start | bytes 73732
  502.3 9.1 %collective-permute-start.22 = (f32[2,96,512]{2,1,0:T(8,128)S(1)}, f32[2,96,512]{2,1,0:T(8,128)S(1)}, u32[]{:S(2)}, u32[]{:S(2)}) collective-permute-start(f32[2,96,512]{2,1,0:T(8,128)S(1)} %slice_add_fusion.2), channel_id=1, source_target_pairs={{1,0},{2,1},{3,2},{4,3},{5,4},{6,5},{7,6},{8,7},{9,8},{10,9},{11,1... | collective-permute-start | bytes 1179656 | tf_op jit(solution)/shard_map/ppermute | solution.py:20
  505.4 10.2 %collective-permute-start.17 = (f32[2,96,512]{2,1,0:T(8,128)S(1)}, f32[2,96,512]{2,1,0:T(8,128)S(1)}, u32[]{:S(2)}, u32[]{:S(2)}) collective-permute-start(f32[2,96,512]{2,1,0:T(8,128)S(1)} %slice_add_fusion.7), channel_id=1, source_target_pairs={{1,0},{2,1},{3,2},{4,3},{5,4},{6,5},{7,6},{8,7},{9,8},{10,9},{11,1... | collective-permute-start | bytes 1179656 | tf_op jit(solution)/shard_map/ppermute | solution.py:20
  513.2 9.9 %collective-permute-start.23 = (f32[2,96,512]{2,1,0:T(8,128)}, f32[2,96,512]{2,1,0:T(8,128)}, u32[]{:S(2)}, u32[]{:S(2)}) collective-permute-start(f32[2,96,512]{2,1,0:T(8,128)} %slice_add_fusion.1), channel_id=1, source_target_pairs={{1,0},{2,1},{3,2},{4,3},{5,4},{6,5},{7,6},{8,7},{9,8},{10,9},{11,1... | collective-permute-start | bytes 1179656 | tf_op jit(solution)/shard_map/ppermute | solution.py:20
  525.0 15.2 %copy-start.23 = (f32[2,96]{1,0:T(2,128)S(1)}, f32[2,96]{1,0:T(2,128)}, u32[]{:S(2)}) copy-start(f32[2,96]{1,0:T(2,128)} %copy-done.21) | copy-start | bytes 2308
  525.0 15.2 %copy-start.26 = (f32[2]{0:T(128)S(1)}, f32[2]{0:T(128)}, u32[]{:S(2)}) copy-start(f32[2]{0:T(128)} %param.16) | copy-start | bytes 28
  (11 other events, 31.5 us)
Sparse Core Ops, SparseCore 0:
  9.4 225.4 all-gather.1
  544.7 38.0 reduce-scatter.3
where the time goes:
time: 600 us; the launch traced here: 590 us
  blocking collectives  243 us (40%)
  matrix products  97.4 us (16%)
  starting transfers between devices  69.9 us (12%)
  local copies, waits for them, and re-layouts  60.5 us (10%)
  waiting for transfers between devices  54.4 us (9%)
  other arithmetic  49.1 us (8%)
  between operations  15.9 us (3%)
    unnamed x2, blocking collectives  232 us
    ppermute x24, starting transfers between devices, passed_along(): return lax.ppermute(array, axis, pairs)  55.1 us
    reduce_scatter x1, waiting for transfers between devices, per_device(): lax.psum_scatter(partial_value, 'step', scatter_dimension=1, tiled=True)  38.2 us
    dot_general x1, matrix products, per_device(): jnp.einsum('sgaqk,sqgae->skge', score_grad, query_split, preferred_elemen...  33.2 us
    dot_general x1, matrix products, per_device(): jnp.einsum('sgaqk,skge->sqgae', score_grad, key_all, preferred_element_ty...  24.8 us
    gather x1, local copies, waits for them, and re-layouts, per_device(): picked = jnp.take(embed_table, jnp.clip(local, 0, shard_rows - 1), axis=0)  22.4 us
    unnamed x80, local copies, waits for them, and re-layouts  18 us
    ppermute x24, waiting for transfers between devices, passed_along(): return lax.ppermute(array, axis, pairs)  16.2 us
  transfers between devices with their start and end apart: 28, of which 9 were waited for; matrix products, arithmetic and copies ran while one was open for 54% of the time, Pallas kernels for 0%

commit v1 on v0

--- a/solution.py
+++ b/solution.py
@@ -1,8 +1,10 @@
+import functools
 import math
 
 import jax
 import jax.numpy as jnp
 from jax import lax
+from jax.experimental import pallas as pl
 from jax.sharding import PartitionSpec as P
 
 HEAD = 128
@@ -49,7 +51,7 @@
     )
 
 
-def per_device(
+def token_split(
     token_ids,
     positions,
     embed_table,
@@ -198,6 +200,258 @@
     return lax.psum_scatter(partial_value, "step", scatter_dimension=1, tiled=True)
 
 
+def attend_kernel(scale, reach, q_ref, p_ref, k_ref, v_ref, low_ref, dq_ref, dk_ref, dv_ref):
+    rows = q_ref.shape[2]
+    span = k_ref.shape[2]
+    heads = q_ref.shape[3] // HEAD
+    keys = k_ref[0, 0]
+    values = v_ref[0, 0]
+    across = (((1,), (1,)), ((), ()))
+    down = (((0,), (0,)), ((), ()))
+    back = lax.broadcasted_iota(jnp.int32, (rows, span), 1) - reach - lax.broadcasted_iota(
+        jnp.int32, (rows, span), 0
+    )
+    visible = (back <= 0) & (back >= -low_ref[0])
+    key_sum = jnp.zeros((span, HEAD), jnp.float32)
+    value_sum = jnp.zeros((span, HEAD), jnp.float32)
+    for head in range(heads):
+        cols = slice(head * HEAD, (head + 1) * HEAD)
+        query = q_ref[0, 0, :, cols]
+        probe = p_ref[0, :, cols]
+        scores = lax.dot_general(query, keys, across, preferred_element_type=jnp.float32) * scale
+        scores = jnp.where(visible, scores, MASKED)
+        powers = jnp.exp(scores - jnp.max(scores, axis=-1, keepdims=True))
+        attention = powers / jnp.sum(powers, axis=-1, keepdims=True)
+        grads = lax.dot_general(probe, values, across, preferred_element_type=jnp.float32)
+        row_dot = jnp.sum(attention * grads, axis=-1, keepdims=True)
+        score_grad = (attention * (grads - row_dot) * scale).astype(jnp.bfloat16)
+        dq_ref[0, 0, :, cols] = jnp.dot(score_grad, keys, preferred_element_type=jnp.float32)
+        key_sum += lax.dot_general(score_grad, query, down, preferred_element_type=jnp.float32)
+        value_sum += lax.dot_general(
+            attention.astype(jnp.bfloat16), probe, down, preferred_element_type=jnp.float32
+        )
+    dk_ref[0, 0] = key_sum
+    dv_ref[0, 0] = value_sum
+
+
+def attend_back(queries, probes, key_win, value_win, positions, reach):
+    steps, blocks, rows, cols = queries.shape
+    span = key_win.shape[2]
+    low = positions[:, :, None]
+    whole = lambda *tail: pl.BlockSpec((1, 1) + tail, lambda j, s: (s, j, 0, 0))
+    shapes = [(rows, cols), (span, HEAD), (span, HEAD)]
+    return pl.pallas_call(
+        functools.partial(attend_kernel, 1.0 / math.sqrt(HEAD), reach),
+        grid=(blocks, steps),
+        in_specs=[
+            whole(rows, cols),
+            pl.BlockSpec((1, rows, cols), lambda j, s: (j, 0, 0)),
+            whole(span, HEAD),
+            whole(span, HEAD),
+            pl.BlockSpec((1, rows, 1), lambda j, s: (j, 0, 0)),
+        ],
+        out_specs=[whole(*shape) for shape in shapes],
+        out_shape=[
+            jax.ShapeDtypeStruct((steps, blocks) + shape, jnp.float32) for shape in shapes
+        ],
+        cost_estimate=pl.CostEstimate(
+            flops=10 * steps * blocks * rows * cols * span,
+            bytes_accessed=4 * steps * blocks * (rows * cols * 2 + span * HEAD * 4),
+            transcendentals=steps * blocks * rows * (cols // HEAD) * span,
+        ),
+    )(queries, probes, key_win, value_win, low)
+
+
+def joined_halves(own, other, index):
+    first = index == 0
+    return jnp.concatenate(
+        [jnp.where(first, own, other), jnp.where(first, other, own)], axis=-1
+    )
+
+
+def head_split(
+    token_ids,
+    positions,
+    embed_table,
+    norm_gain,
+    query_weight,
+    key_weight,
+    value_weight,
+    path_points,
+    probe_direction,
+):
+    seq_len = token_ids.shape[0]
+    steps = path_points.shape[0]
+    outer = key_weight.shape[1] // HEAD
+    group = query_weight.shape[1] // key_weight.shape[1]
+    group_cols = group * HEAD
+    seq_index = lax.axis_index("seq")
+    seq_count = lax.axis_size("seq")
+    step_index = lax.axis_index("step")
+    inner = seq_count // outer
+    mine = seq_index % inner
+    far = seq_index // inner
+    far_groups = [[o * inner + i for o in range(outer)] for i in range(inner)]
+    near_groups = [[o * inner + i for i in range(inner)] for o in range(outer)]
+    swap = [(0, 1), (1, 0)]
+
+    both = lax.all_gather(jnp.stack([token_ids, positions]), "seq", axis=0)
+    ids_all = both[:, 0]
+    block_positions = lax.dynamic_index_in_dim(
+        both[:, 1].reshape(outer, inner, seq_len), mine, 1, keepdims=False
+    )
+
+    split = lambda array: array.reshape(array.shape[0], outer, -1)
+    joined = jnp.concatenate([split(query_weight), split(key_weight), split(value_weight)], axis=2)
+    joined = joined.transpose(1, 0, 2)
+    traded = [lax.dynamic_index_in_dim(joined, far, 0, keepdims=False)]
+    for by in range(1, outer):
+        block = lax.dynamic_index_in_dim(joined, (far + by) % outer, 0, keepdims=False)
+        ring = [(d, (d + by * inner) % seq_count) for d in range(seq_count)]
+        traded.append(lax.ppermute(block, "seq", ring))
+    traded = jnp.stack(traded)
+    crossed = lax.ppermute(traded, "seq", [(d, d ^ 2) for d in range(seq_count)])
+    side = [(d, d ^ 1) for d in range(seq_count)]
+    flipped = [
+        traded,
+        lax.ppermute(traded, "seq", side),
+        crossed,
+        lax.ppermute(crossed, "seq", side),
+    ]
+    flipped = jnp.stack(flipped)
+    weights = jnp.concatenate(
+        [
+            lax.dynamic_slice(
+                flipped, (mine ^ i, (far - o) % outer, 0, 0), (1, 1) + flipped.shape[2:]
+            ).reshape(flipped.shape[2:])
+            for o in range(outer)
+            for i in range(inner)
+        ],
+        axis=0,
+    )
+    probes = lax.all_to_all(
+        split(probe_direction).transpose(1, 0, 2), "seq", 0, 0, axis_index_groups=far_groups
+    )
+
+    wanted = jnp.pad(ids_all, ((0, 0), (0, 16))).reshape(-1)
+    shard_rows = embed_table.shape[0]
+    local = wanted - seq_index * shard_rows
+    owned = (local >= 0) & (local < shard_rows)
+    picked = jnp.take(embed_table, jnp.clip(local, 0, shard_rows - 1), axis=0)
+    own_columns = lax.psum_scatter(
+        jnp.where(owned[:, None], picked, jnp.zeros((), jnp.bfloat16)),
+        "seq",
+        scatter_dimension=0,
+        tiled=True,
+    )
+    middle = seq_len // 2
+    late = own_columns[:middle]
+    late = joined_halves(late, lax.ppermute(late, "step", swap), step_index)
+    early = lax.all_gather(own_columns[middle:], "seq", axis=0, axis_index_groups=far_groups)
+    late = lax.all_gather(late, "seq", axis=0, axis_index_groups=far_groups)
+    early = joined_halves(early, lax.ppermute(early, "step", swap), step_index)
+    looked = jnp.concatenate([late, early[:, : seq_len - middle]], axis=1)
+    features = looked.shape[2]
+    embedded = looked.reshape(outer * seq_len, features).astype(jnp.float32)
+    baseline = early[0, seq_len - middle : seq_len - middle + 1].astype(jnp.float32)
+    rows = outer * seq_len
+
+    difference = embedded - baseline
+    inputs = baseline[None] + path_points[:, None, None] * difference[None]
+    radius = jnp.sqrt(jnp.mean(inputs * inputs, axis=-1, keepdims=True) + NORM_EPSILON)
+    unitized = inputs / radius
+    normed = (unitized * norm_gain).astype(jnp.bfloat16).reshape(steps * rows, features)
+    projected = jnp.dot(normed, weights, preferred_element_type=jnp.float32)
+    projected = projected.reshape(steps, rows, -1)
+    cosine, sinusoid = rope_tables(block_positions.reshape(rows), HEAD)
+    queries = rotate(
+        projected[..., :group_cols].reshape(steps, rows, group, HEAD), cosine, sinusoid
+    ).astype(jnp.bfloat16)
+    key_rows = rotate(
+        projected[..., group_cols : group_cols + HEAD].reshape(steps, rows, 1, HEAD),
+        cosine,
+        sinusoid,
+    ).astype(jnp.bfloat16)
+    value_rows = projected[..., group_cols + HEAD :].astype(jnp.bfloat16)
+    shared = jnp.concatenate([key_rows.reshape(steps, rows, HEAD), value_rows], axis=2)
+    shared = lax.all_gather(
+        shared.reshape(steps, outer, seq_len, 2 * HEAD),
+        "seq",
+        axis=0,
+        axis_index_groups=near_groups,
+    )
+    shared = shared.transpose(1, 2, 0, 3, 4).reshape(steps, seq_count * seq_len, 2 * HEAD)
+    shared = jnp.pad(shared, ((0, 0), (REACH * seq_len, 0), (0, 0)))
+    span = (REACH + 1) * seq_len
+    starts = [(o * inner + mine) * seq_len for o in range(outer)]
+    windows = jnp.stack(
+        [lax.dynamic_slice_in_dim(shared, start, span, 1) for start in starts], axis=1
+    )
+    query_grad, key_grad, value_grad = attend_back(
+        queries.reshape(steps, outer, seq_len, group_cols),
+        probes,
+        windows[..., :HEAD],
+        windows[..., HEAD:],
+        block_positions,
+        REACH * seq_len,
+    )
+    pairs = jnp.concatenate([key_grad, value_grad], axis=3)
+    long = outer * inner * seq_len
+    shifted = jnp.zeros((steps, long + REACH * seq_len, 2 * HEAD), jnp.float32)
+    for o in range(outer):
+        held = lax.dynamic_slice_in_dim(shifted, starts[o], span, 1) + pairs[:, o]
+        shifted = lax.dynamic_update_slice_in_dim(shifted, held, starts[o], 1)
+    spread = shifted[:, REACH * seq_len :].reshape(steps, outer, inner, seq_len, 2 * HEAD)
+    spread = spread.transpose(2, 0, 1, 3, 4).reshape(2, 2, steps * rows, 2 * HEAD)
+    kept = lax.dynamic_index_in_dim(spread, mine % 2, 1, keepdims=False)
+    sent = lax.dynamic_index_in_dim(spread, 1 - mine % 2, 1, keepdims=False)
+    kept = kept + lax.ppermute(sent, "seq", side)
+    sent = lax.dynamic_index_in_dim(kept, 1 - mine // 2, 0, keepdims=False)
+    kept = lax.dynamic_index_in_dim(kept, mine // 2, 0, keepdims=False)
+    total = kept + lax.ppermute(sent, "seq", [(d, d ^ 2) for d in range(seq_count)])
+    total = total.reshape(steps, rows, 2 * HEAD)
+    query_back = unrotate(query_grad.reshape(steps, rows, group, HEAD), cosine, sinusoid)
+    key_back = unrotate(total[..., :HEAD].reshape(steps, rows, 1, HEAD), cosine, sinusoid)
+    joined_grad = jnp.concatenate(
+        [
+            query_back.reshape(steps, rows, group_cols).astype(jnp.bfloat16),
+            key_back.reshape(steps, rows, HEAD).astype(jnp.bfloat16),
+            total[..., HEAD:].astype(jnp.bfloat16),
+        ],
+        axis=2,
+    ).reshape(steps * rows, -1)
+    contract = (((1,), (1,)), ((), ()))
+    norm_grad = lax.dot_general(
+        joined_grad, weights, contract, preferred_element_type=jnp.float32
+    ).reshape(steps, rows, features)
+    scaled = norm_gain * norm_grad
+    input_grad = (scaled - unitized * jnp.mean(scaled * unitized, axis=-1, keepdims=True)) / radius
+    partial_value = difference * jnp.sum(input_grad, axis=0) / steps
+    part = features // 2
+    stacked = partial_value.reshape(outer, seq_len, features)
+    pieces = []
+    for begin, end in ((0, middle), (middle, seq_len)):
+        piece = stacked[:, begin:end]
+        kept = lax.dynamic_slice_in_dim(piece, step_index * part, part, 2)
+        given = lax.dynamic_slice_in_dim(piece, (1 - step_index) * part, part, 2)
+        arrived = lax.ppermute(given.astype(jnp.bfloat16), "step", swap)
+        halved = (kept + arrived.astype(jnp.float32)).astype(jnp.bfloat16)
+        pieces.append(
+            lax.psum_scatter(
+                halved, "seq", scatter_dimension=0, axis_index_groups=far_groups
+            ).astype(jnp.float32)
+        )
+    return jnp.concatenate(pieces, axis=0)
+
+
+def per_device(*args):
+    shared_heads = args[5].shape[1] // HEAD
+    fits = shared_heads > 1 and lax.axis_size("seq") == 4 * shared_heads
+    if fits and lax.axis_size("step") == 2:
+        return head_split(*args)
+    return token_split(*args)
+
+
 def solution(mesh):
     in_specs = (
         P("seq"),

time: 600 us -> 441 us (0.73)
  blocking collectives: 243 us -> 23.1 us
  waiting for transfers between devices: 54.4 us -> 221 us
  matrix products: 97.4 us -> 18.5 us
  starting transfers between devices: 69.9 us -> 15.4 us
  Pallas kernels: 0 us -> 23.3 us
  local copies, waits for them, and re-layouts: 60.5 us -> 72.6 us
    unnamed x2 -> x0, blocking collectives: 232 us -> none
    ppermute x24 -> x12, waiting for transfers between devices: 16.2 us -> 138 us  [the longest x1 46.9 us: head_split(): lax.ppermute(traded, 'seq', [(d, d ^ 2) for d in range(seq_count)])]
    dot_general x7 -> x2, matrix products: 97.4 us -> 18.5 us  [the longest x1 12.8 us: head_split(): lax.dot_general(joined_grad, weights, contract, preferred_element_type=jn...]
    ppermute x24 -> x12, starting transfers between devices: 55.1 us -> 10.7 us  [the longest x3 3.99 us: head_split(): traded.append(lax.ppermute(block, 'seq', ring))]
    all_gather x1 -> x3, waiting for transfers between devices: 0.02 us -> 35.1 us  [the longest x1 17.4 us: head_split(): lax.all_gather(own_columns[middle:], 'seq', axis=0, axis_index_groups=far...]
    pallas_call x0 -> x1, Pallas kernels: none -> 23.3 us  [attend_back(): pl.pallas_call(functools.partial(attend_kernel, 1.0 / math.sqrt(HEAD), re...]
    unnamed x2 -> x0, starting transfers between devices: 14.8 us -> none
    all_gather x1, blocking collectives: 10.7 us -> 23.1 us  [head_split(): both = lax.all_gather(jnp.stack([token_ids, positions]), 'seq', axis=0)]
  transfers between devices with their start and end apart: 28 -> 19, of which waited for: 9 -> 15; matrix products, arithmetic and copies ran while one was open for 54% -> 11% of each run, Pallas kernels for 0% -> 0%
where the time goes in v1:
time: 441 us; the launch traced here: 433 us
  waiting for transfers between devices  221 us (50%)
  local copies, waits for them, and re-layouts  72.6 us (16%)
  other arithmetic  44.4 us (10%)
  Pallas kernels  23.3 us (5%)
  blocking collectives  23.1 us (5%)
  matrix products  18.5 us (4%)
  starting transfers between devices  15.4 us (3%)
  between operations  14.9 us (3%)
    ppermute x1, waiting for transfers between devices, head_split(): lax.ppermute(traded, 'seq', [(d, d ^ 2) for d in range(seq_count)])  46.9 us
    ppermute x2, waiting for transfers between devices, head_split(): arrived = lax.ppermute(given.astype(jnp.bfloat16), 'step', swap)  34.1 us
    reduce_scatter x2, waiting for transfers between devices, head_split(): lax.psum_scatter(halved, 'seq', scatter_dimension=0, axis_index_groups=fa...  28.8 us
    ppermute x3, waiting for transfers between devices, head_split(): traded.append(lax.ppermute(block, 'seq', ring))  28.2 us
    unnamed x75, local copies, waits for them, and re-layouts  24.3 us
    pallas_call x1, Pallas kernels, attend_back(): pl.pallas_call(functools.partial(attend_kernel, 1.0 / math.sqrt(HEAD), re...  23.3 us
    all_gather x1, blocking collectives, head_split(): both = lax.all_gather(jnp.stack([token_ids, positions]), 'seq', axis=0)  23.1 us
    gather x1, local copies, waits for them, and re-layouts, head_split(): picked = jnp.take(embed_table, jnp.clip(local, 0, shard_rows - 1), axis=0)  22.3 us
  transfers between devices with their start and end apart: 19, of which 15 were waited for; matrix products, arithmetic and copies ran while one was open for 11% of the time, Pallas kernels for 0%

profile of v1, /device:TPU:0, one launch (start us, length us, event | category | flops | bytes accessed | tf_op | source)
XLA Modules:
  0.0 432.9 jit_solution(13191179990851727039)
XLA Ops:
  7.2 23.1 %all-gather.3 = s32[16,2,96]{2,1,0:T(2,128)S(1)} all-gather(s32[1,2,96]{2,1,0:T(2,128)S(1)} %add_bitcast_fusion), channel_id=2, replica_groups=mesh['step'=2,'seq'=16] {'seq'}, dimensions={0}, use_global_device_ids=true | all-gather | bytes 13056 | tf_op jit(solution)/shard_map/all_gather | solution.py:298
  30.7 22.3 %gather_fusion = bf16[1792,2048]{1,0:T(8,128)(2,1)} fusion(bf16[4008,2048]{1,0:T(8,128)(2,1)} %param.11, s32[2048]{0:T(1024)S(1)} %pad_clamp_fusion), kind=kCustom, calls=%fused_computation | custom fusion | bytes 14687232 | tf_op jit(solution)/shard_map/jit(_take)/gather | solution.py:340
  53.0 7.0 %select_select_fusion = bf16[1792,2048]{1,0:T(8,128)(2,1)} fusion(bf16[1792,2048]{1,0:T(8,128)(2,1)} %gather_fusion, pred[1792]{0:T(1024)(128)(4,1)S(1)} %compare_and_fusion, pred[1792]{0:T(1024)(128)(4,1)S(1)} %and.80), kind=kLoop, calls=%fused_computation.7 | loop fusion | flops 7340032 | bytes 14683648 | tf_op jit(solution)/shard_map/jit(_where)/select_n | solution.py:342
  63.1 3.9 collective-permute-start.4
  67.1 9.4 %collective-permute-done.2 = bf16[256,768]{1,0:T(8,128)(2,1)S(1)} collective-permute-done((bf16[256,768]{1,0:T(8,128)(2,1)S(1)}, bf16[256,768]{1,0:T(8,128)(2,1)S(1)}, u32[]{:S(2)}, u32[]{:S(2)}) %collective-permute-start.2) | collective-permute-done | bytes 393248 | tf_op jit(solution)/shard_map/ppermute | solution.py:311
  76.5 18.8 %collective-permute-done.3 = bf16[256,768]{1,0:T(8,128)(2,1)S(1)} collective-permute-done((bf16[256,768]{1,0:T(8,128)(2,1)S(1)}, bf16[256,768]{1,0:T(8,128)(2,1)S(1)}, u32[]{:S(2)}, u32[]{:S(2)}) %collective-permute-start.3) | collective-permute-done | bytes 393248 | tf_op jit(solution)/shard_map/ppermute | solution.py:311
  96.9 46.9 %collective-permute-done.6 = bf16[4,256,768]{2,1,0:T(8,128)(2,1)S(1)} collective-permute-done((bf16[4,256,768]{2,1,0:T(8,128)(2,1)}, bf16[4,256,768]{2,1,0:T(8,128)(2,1)S(1)}, u32[]{:S(2)}, u32[]{:S(2)}) %collective-permute-start.6) | collective-permute-done | bytes 1572896 | tf_op jit(solution)/shard_map/ppermute | solution.py:313
  145.2 18.7 %reduce-scatter.4.cloned.1.call-done = bf16[112,2048]{1,0:T(8,128)(2,1)} async-done(((bf16[1792,2048]{1,0:T(8,128)(2,1)}), bf16[112,2048]{1,0:T(8,128)(2,1)}) %reduce-scatter.4.cloned.1.call-update) | async-done | bytes 458768 | tf_op jit(solution)/shard_map/reduce_scatter | solution.py:341
  163.9 1.7 slice.118
  165.7 3.0 pad_maximum_fusion
  171.4 3.5 collective-permute-done
  175.0 17.4 %all-gather.12.cloned.1.call-done = bf16[256,2048]{1,0:T(8,128)(2,1)} async-done(((bf16[64,2048]{1,0:T(8,128)(2,1)}), bf16[256,2048]{1,0:T(8,128)(2,1)}) %all-gather.12.cloned.1.call-update) | async-done | bytes 1048592 | tf_op jit(solution)/shard_map/all_gather | solution.py:350
  194.9 1.8 bitcast_dynamic-update-slice_fusion.7
  196.7 1.8 bitcast_dynamic-update-slice_fusion.6
  198.5 1.8 bitcast_dynamic-update-slice_fusion.5
  200.3 1.8 bitcast_dynamic-update-slice_fusion.4
  202.1 1.8 bitcast_dynamic-update-slice_fusion.3
  203.9 1.8 bitcast_dynamic-update-slice_fusion.2
  205.7 1.8 bitcast_dynamic-update-slice_fusion.1
  207.5 1.8 bitcast_dynamic-update-slice_fusion
  209.3 7.8 %collective-permute-done.1 = bf16[4,64,2048]{2,1,0:T(8,128)(2,1)S(1)} collective-permute-done((bf16[4,64,2048]{2,1,0:T(8,128)(2,1)}, bf16[4,64,2048]{2,1,0:T(8,128)(2,1)S(1)}, u32[]{:S(2)}, u32[]{:S(2)}) %collective-permute-start.1) | collective-permute-done | bytes 1048608 | tf_op jit(solution)/shard_map/ppermute | solution.py:352
  217.3 13.1 %all-gather.10.cloned.1.call-done = bf16[192,4096]{1,0:T(8,128)(2,1)} async-done(((bf16[48,4096]{1,0:T(8,128)(2,1)}), bf16[192,4096]{1,0:T(8,128)(2,1)}) %all-gather.10.cloned.1.call-update) | async-done | bytes 1572880 | tf_op jit(solution)/shard_map/all_gather | solution.py:351
  230.4 2.3 maximum_convert_fusion
  233.9 1.9 multiply_reduce_fusion.1
  235.8 5.6 %fusion.1 = f32[2,384,768]{2,1,0:T(8,128)S(1)} fusion(bf16[4096,768]{1,0:T(8,128)(2,1)S(1)} %bitcast.182, f32[2,384]{1,0:T(2,128)S(1)} %add_sqrt_fusion, f32[384,4096]{1,0:T(8,128)S(1)} %bitcast_subtract_fusion, f32[2]{0:T(128)S(1)} %copy-done.22, f32[4096]{0:T(1024)S(1)} %bitcast.166, f32[4096]{0:T(1024)S(1)} %copy-done.18), kind=kOutput, calls=%fused_computation.8 | convolution fusion | flops 4847566848 | bytes 14978056 | tf_op jit(solution)/shard_map/dot_general | solution.py:364
  244.6 4.1 all-to-all-start
  249.9 2.9 slice.121
  252.8 1.8 reshape.346
  257.9 4.5 %all-gather.8.cloned.1.call-done = bf16[4,2,4,96,256]{4,3,2,1,0:T(8,128)(2,1)} async-done(((bf16[1,2,4,96,256]{4,3,2,1,0:T(8,128)(2,1)}), bf16[4,2,4,96,256]{4,3,2,1,0:T(8,128)(2,1)}) %all-gather.8.cloned.1.call-update) | async-done | bytes 1572880 | tf_op jit(solution)/shard_map/all_gather | solution.py:377
  264.0 1.8 fusion.23
  266.2 2.1 fusion.33
  268.4 23.3 %shard_map.91 = (f32[2,4,96,512]{3,2,1,0:T(8,128)}, f32[2,4,672,128]{3,2,1,0:T(8,128)}, f32[2,4,672,128]{3,2,1,0:T(8,128)}) custom-call(bf16[2,4,96,512]{3,2,1,0:T(8,128)(2,1)} %convert_element_type.102.q_ref, bf16[4,96,512]{2,1,0:T(8,128)(2,1)} %all-to-all-done.p_ref, bf16[2,4,672,128]{3,2,1,0:T(8,128)(2,1)} %get-tuple-element.14.k_ref, ...), custom_call_target="tpu_custom_call" | custom-call | flops 2642411520 | bytes 14155776 | tf_op jit(solution)/shard_map/pallas_call | solution.py:243
  291.6 2.2 constant_dynamic-update-slice_fusion.1
  296.3 1.6 copy-done.2
  299.4 3.4 collective-permute-done.8
  302.8 1.6 bitcast_add_fusion
  306.9 2.0 reshape.350
  312.3 14.2 %collective-permute-done.9 = f32[768,256]{1,0:T(8,128)} collective-permute-done((f32[768,256]{1,0:T(8,128)}, f32[768,256]{1,0:T(8,128)}, u32[]{:S(2)}, u32[]{:S(2)}) %collective-permute-start.9) | collective-permute-done | bytes 786464 | tf_op jit(solution)/shard_map/ppermute | solution.py:411
  328.5 12.8 %multiply_reduce_fusion = (f32[2,384]{1,0:T(2,128)S(1)}, f32[2,384,4096]{2,1,0:T(8,128)}) fusion(f32[2,384]{1,0:T(2,128)S(1)} %copy-done.21, f32[384,4096]{1,0:T(8,128)} %copy-done, f32[2]{0:T(128)S(1)} %copy-done.23, f32[4096]{0:T(1024)S(1)} %bitcast.167, f32[4096]{0:T(1024)S(1)} %copy-done.19, bf16[4096,768]{1,0:T(8,128)(2,1)} %bitcast_dynamic-update-slice_fusion, ...), kind=kOutput, calls=%fused_computation.2 | convolution fusion | flops 4854250496 | bytes 26384392 | tf_op jit(solution)/shard_map/dot_general | solution.py:424
  341.4 7.9 %divide_reduce_fusion = f32[384,4096]{1,0:T(8,128)S(1)} fusion(f32[2,384,4096]{2,1,0:T(8,128)} %get-tuple-element.42, f32[2,384]{1,0:T(2,128)S(1)} %broadcast_multiply_fusion, f32[2,384]{1,0:T(2,128)S(1)} %copy-done.21, f32[384,4096]{1,0:T(8,128)S(1)} %bitcast.144, f32[2]{0:T(128)S(1)} %copy-done.23, f32[4096]{0:T(1024)S(1)} %bitcast.168, f32[4096]{0:T(1024)S(1)} %copy-done.19), kind=kLoop, calls=%fused_computation.1 | loop fusion | flops 23592960 | bytes 25204744 | tf_op jit(solution)/shard_map/reduce_sum | solution.py:429
  351.0 1.6 copy-done.3
  355.1 17.7 %collective-permute-done.10 = bf16[4,48,2048]{2,1,0:T(8,128)(2,1)} collective-permute-done((bf16[4,48,2048]{2,1,0:T(8,128)(2,1)}, bf16[4,48,2048]{2,1,0:T(8,128)(2,1)}, u32[]{:S(2)}, u32[]{:S(2)}) %collective-permute-start.10) | collective-permute-done | bytes 786464 | tf_op jit(solution)/shard_map/ppermute | solution.py:437
  372.8 2.7 add_convert_fusion.1
  375.7 1.6 collective-permute-start.11
  377.2 16.5 %collective-permute-done.11 = bf16[4,48,2048]{2,1,0:T(8,128)(2,1)S(1)} collective-permute-done((bf16[4,48,2048]{2,1,0:T(8,128)(2,1)S(1)}, bf16[4,48,2048]{2,1,0:T(8,128)(2,1)S(1)}, u32[]{:S(2)}, u32[]{:S(2)}) %collective-permute-start.11) | collective-permute-done | bytes 786464 | tf_op jit(solution)/shard_map/ppermute | solution.py:437
  394.8 4.0 reduce-scatter.6.cloned.1.call-done
  398.8 24.8 %reduce-scatter.8.cloned.1.call-done = bf16[1,48,2048]{2,1,0:T(8,128)(2,1)} async-done(((bf16[4,48,2048]{2,1,0:T(8,128)(2,1)}), bf16[1,48,2048]{2,1,0:T(8,128)(2,1)}) %reduce-scatter.8.cloned.1.call-update) | async-done | bytes 196624 | tf_op jit(solution)/shard_map/reduce_scatter | solution.py:440
  423.7 2.0 maximum_convert_fusion.1
  (158 shorter events, 40.0 us)
Async XLA Ops:
  6.5 157.4 %reduce-scatter.4.cloned.1.call-start = ((), (), s32[]{:S(2)}) async-start(), calls=%async_computation.4 | async-start | bytes 7798784 | tf_op jit(solution)/shard_map/reduce_scatter | solution.py:341
  60.1 1.2 copy-start.9
  60.1 1.7 copy-start.13
  60.1 1.9 copy-start.14
  60.1 132.3 %all-gather.12.cloned.1.call-start = ((), (), s32[]{:S(2)}) async-start(), calls=%async_computation.9 | async-start | bytes 1310720 | tf_op jit(solution)/shard_map/all_gather | solution.py:350
  62.6 14.0 %collective-permute-start.2 = (bf16[256,768]{1,0:T(8,128)(2,1)S(1)}, bf16[256,768]{1,0:T(8,128)(2,1)S(1)}, u32[]{:S(2)}, u32[]{:S(2)}) collective-permute-start(bf16[256,768]{1,0:T(8,128)(2,1)S(1)} %bitcast.174), channel_id=1, source_target_pairs={{0,4},{1,5},{2,6},{3,7},{4,8},{5,9},{6,10},{7,11},{8,12},{9,13},{1... | collective-permute-start | bytes 1179656 | tf_op jit(solution)/shard_map/ppermute | solution.py:311
  62.8 32.5 %collective-permute-start.3 = (bf16[256,768]{1,0:T(8,128)(2,1)S(1)}, bf16[256,768]{1,0:T(8,128)(2,1)S(1)}, u32[]{:S(2)}, u32[]{:S(2)}) collective-permute-start(bf16[256,768]{1,0:T(8,128)(2,1)S(1)} %bitcast.175), channel_id=1, source_target_pairs={{0,8},{1,9},{2,10},{3,11},{4,12},{5,13},{6,14},{7,15},{8,0},{9,1},... | collective-permute-start | bytes 1179656 | tf_op jit(solution)/shard_map/ppermute | solution.py:311
  63.1 32.3 %collective-permute-start.4 = (bf16[256,768]{1,0:T(8,128)(2,1)S(1)}, bf16[256,768]{1,0:T(8,128)(2,1)S(1)}, u32[]{:S(2)}, u32[]{:S(2)}) collective-permute-start(bf16[256,768]{1,0:T(8,128)(2,1)S(1)} %bitcast.176), channel_id=1, source_target_pairs={{0,12},{1,13},{2,14},{3,15},{4,0},{5,1},{6,2},{7,3},{8,4},{9,5},{1... | collective-permute-start | bytes 1179656 | tf_op jit(solution)/shard_map/ppermute | solution.py:311
  96.9 46.9 %collective-permute-start.6 = (bf16[4,256,768]{2,1,0:T(8,128)(2,1)}, bf16[4,256,768]{2,1,0:T(8,128)(2,1)S(1)}, u32[]{:S(2)}, u32[]{:S(2)}) collective-permute-start(bf16[4,256,768]{2,1,0:T(8,128)(2,1)} %get-tuple-element.26), channel_id=1, source_target_pairs={{0,2},{1,3},{2,0},{3,1},{4,6},{5,7},{6,4},{7,5},{8,10},{9,11},{10,... | collective-permute-start | bytes 4718600 | tf_op jit(solution)/shard_map/ppermute | solution.py:313
  96.9 68.8 %collective-permute-start.5 = (bf16[4,256,768]{2,1,0:T(8,128)(2,1)}, bf16[4,256,768]{2,1,0:T(8,128)(2,1)}, u32[]{:S(2)}, u32[]{:S(2)}) collective-permute-start(bf16[4,256,768]{2,1,0:T(8,128)(2,1)} %get-tuple-element.26), channel_id=1, source_target_pairs={{0,1},{1,0},{2,3},{3,2},{4,5},{5,4},{6,7},{7,6},{8,9},{9,8},{10,11... | collective-permute-start | bytes 4718600 | tf_op jit(solution)/shard_map/ppermute | solution.py:317
  143.7 21.9 %collective-permute-start.7 = (bf16[4,256,768]{2,1,0:T(8,128)(2,1)S(1)}, bf16[4,256,768]{2,1,0:T(8,128)(2,1)}, u32[]{:S(2)}, u32[]{:S(2)}) collective-permute-start(bf16[4,256,768]{2,1,0:T(8,128)(2,1)S(1)} %collective-permute-done.6), channel_id=1, source_target_pairs={{0,1},{1,0},{2,3},{3,2},{4,5},{5,4},{6,7},{7,6},{8,9},{9,8},{10,11... | collective-permute-start | bytes 4718600 | tf_op jit(solution)/shard_map/ppermute | solution.py:319
  143.8 0.6 copy-start.16
  165.6 64.9 %all-gather.10.cloned.1.call-start = ((), (), s32[]{:S(2)}) async-start(), calls=%async_computation.8 | async-start | bytes 1966080 | tf_op jit(solution)/shard_map/all_gather | solution.py:351
  165.6 3.3 copy-start.10
  168.7 2.7 copy-start.1
  169.0 6.0 %collective-permute-start = (bf16[48,2048]{1,0:T(8,128)(2,1)S(1)}, bf16[48,2048]{1,0:T(8,128)(2,1)S(1)}, u32[]{:S(2)}, u32[]{:S(2)}) collective-permute-start(bf16[48,2048]{1,0:T(8,128)(2,1)S(1)} %slice.117), channel_id=1, source_target_pairs={{0,16},{16,0},{1,17},{17,1},{2,18},{18,2},{3,19},{19,3},{4,20},{20... | collective-permute-start | bytes 589832 | tf_op jit(solution)/shard_map/ppermute | solution.py:349
  171.4 3.6 copy-start.15
  192.4 24.6 %copy-start.8 = (bf16[256,2048]{1,0:T(8,128)(2,1)S(1)}, bf16[256,2048]{1,0:T(8,128)(2,1)}, u32[]{:S(2)}) copy-start(bf16[256,2048]{1,0:T(8,128)(2,1)} %all-gather.12.cloned.1.call-done) | copy-start | bytes 3145732
  192.4 24.6 %collective-permute-start.1 = (bf16[4,64,2048]{2,1,0:T(8,128)(2,1)}, bf16[4,64,2048]{2,1,0:T(8,128)(2,1)S(1)}, u32[]{:S(2)}, u32[]{:S(2)}) collective-permute-start(bf16[4,64,2048]{2,1,0:T(8,128)(2,1)} %bitcast.157), channel_id=1, source_target_pairs={{0,16},{16,0},{1,17},{17,1},{2,18},{18,2},{3,19},{19,3},{4,20},{20... | collective-permute-start | bytes 3145736 | tf_op jit(solution)/shard_map/ppermute | solution.py:352
  194.7 67.8 %all-gather.8.cloned.1.call-start = ((), (), s32[]{:S(2)}) async-start(), calls=%async_computation.5 | async-start | bytes 1966080 | tf_op jit(solution)/shard_map/all_gather | solution.py:377
  230.4 5.3 %slice-start.2 = ((s8[6291456]{0:T(1024)(128)(4,1)}), s8[4194304]{0:T(1024)(128)(4,1)S(1)}, s32[]{:S(2)}) async-start(s8[6291456]{0:T(1024)(128)(4,1)} %bitcast.181), calls=%async_computation.12 | async-start | bytes 8388608
  232.8 1.1 copy-start.22
  232.8 3.0 slice-start.3
  233.9 7.6 %copy-start = (f32[384,4096]{1,0:T(8,128)}, f32[384,4096]{1,0:T(8,128)S(1)}, u32[]{:S(2)}) copy-start(f32[384,4096]{1,0:T(8,128)S(1)} %bitcast_subtract_fusion) | copy-start | bytes 18874372
  233.9 1.9 copy-start.18
  235.8 5.7 %copy-start.20 = (f32[2,384]{1,0:T(2,128)}, f32[2,384]{1,0:T(2,128)S(1)}, u32[]{:S(2)}) copy-start(f32[2,384]{1,0:T(2,128)S(1)} %add_sqrt_fusion) | copy-start | bytes 9220
  235.8 8.0 %copy-start.12 = (bf16[96,2048]{1,0:T(8,128)(2,1)S(1)}, bf16[96,2048]{1,0:T(8,128)(2,1)}, u32[]{:S(2)}) copy-start(bf16[96,2048]{1,0:T(8,128)(2,1)} %param.17) | copy-start | bytes 1179652
  241.5 1.4 copy-start.7
  241.5 7.6 %copy-start.17 = (s32[4,1,96]{2,1,0:T(1,128)S(1)}, s32[4,1,96]{2,1,0:T(1,128)}, u32[]{:S(2)}) copy-start(s32[4,1,96]{2,1,0:T(1,128)} %copy-done.16) | copy-start | bytes 4612
  244.6 23.7 %all-to-all-start = ((bf16[4,96,512]{2,1,0:T(8,128)(2,1)}), bf16[4,96,512]{2,1,0:T(8,128)(2,1)}, u32[]{:S(2)}, u32[]{:S(2)}) async-start(bf16[4,96,512]{2,1,0:T(8,128)(2,1)} %bitcast.142), calls=%async_computation.1 | async-start | bytes 786432 | tf_op jit(solution)/shard_map/all_to_all | solution.py:332
  248.8 150.0 %reduce-scatter.6.cloned.1.call-start = ((), (), s32[]{:S(2)}) async-start(), calls=%async_computation.6 | async-start | bytes 983040 | tf_op jit(solution)/shard_map/reduce_scatter | solution.py:440
  291.6 2.6 copy-start.6
  296.3 1.6 copy-start.2
  299.2 3.6 collective-permute-start.8
  304.4 1.2 copy-start.5
  306.5 20.0 %collective-permute-start.9 = (f32[768,256]{1,0:T(8,128)}, f32[768,256]{1,0:T(8,128)}, u32[]{:S(2)}, u32[]{:S(2)}) collective-permute-start(f32[768,256]{1,0:T(8,128)} %dynamic-slice_bitcast_fusion.1), channel_id=1, source_target_pairs={{0,2},{1,3},{2,0},{3,1},{4,6},{5,7},{6,4},{7,5},{8,10},{9,11},{10,... | collective-permute-start | bytes 2359304 | tf_op jit(solution)/shard_map/ppermute | solution.py:411
  310.0 18.4 %copy-start.19 = (f32[4096]{0:T(1024)S(1)}, f32[4096]{0:T(1024)}, u32[]{:S(2)}) copy-start(f32[4096]{0:T(1024)} %param.12) | copy-start | bytes 49156
  310.0 18.4 %copy-start.21 = (f32[2,384]{1,0:T(2,128)S(1)}, f32[2,384]{1,0:T(2,128)}, u32[]{:S(2)}) copy-start(f32[2,384]{1,0:T(2,128)} %copy-done.20) | copy-start | bytes 9220
  310.0 18.4 %copy-start.23 = (f32[2]{0:T(128)S(1)}, f32[2]{0:T(128)}, u32[]{:S(2)}) copy-start(f32[2]{0:T(128)} %param.16) | copy-start | bytes 28
  312.3 16.2 %copy-start.11 = (bf16[2,384,512]{2,1,0:T(8,128)(2,1)S(1)}, bf16[2,384,512]{2,1,0:T(8,128)(2,1)}, u32[]{:S(2)}) copy-start(bf16[2,384,512]{2,1,0:T(8,128)(2,1)} %convert_element_type.103) | copy-start | bytes 2359300
  328.0 13.3 %slice-start = ((s8[6291456]{0:T(1024)(128)(4,1)}), s8[4194304]{0:T(1024)(128)(4,1)S(1)}, s32[]{:S(2)}) async-start(s8[6291456]{0:T(1024)(128)(4,1)} %bitcast.143), calls=%async_computation.10 | async-start | bytes 8388608
  328.5 12.9 %slice-start.1 = ((s8[6291456]{0:T(1024)(128)(4,1)}), s8[2097152]{0:T(1024)(128)(4,1)S(1)}, s32[]{:S(2)}) async-start(s8[6291456]{0:T(1024)(128)(4,1)} %bitcast.143), calls=%async_computation.11 | async-start | bytes 4194304
  341.4 7.9 %copy-start.4 = (bf16[192,4096]{1,0:T(8,128)(2,1)S(1)}, bf16[192,4096]{1,0:T(8,128)(2,1)}, u32[]{:S(2)}) copy-start(bf16[192,4096]{1,0:T(8,128)(2,1)} %all-gather.10.cloned.1.call-done) | copy-start | bytes 4718596
  351.0 1.6 copy-start.3
  353.6 19.1 %collective-permute-start.10 = (bf16[4,48,2048]{2,1,0:T(8,128)(2,1)}, bf16[4,48,2048]{2,1,0:T(8,128)(2,1)}, u32[]{:S(2)}, u32[]{:S(2)}) collective-permute-start(bf16[4,48,2048]{2,1,0:T(8,128)(2,1)} %dynamic-slice_convert_fusion.1), channel_id=1, source_target_pairs={{0,16},{16,0},{1,17},{17,1},{2,18},{18,2},{3,19},{19,3},{4,20},{20... | collective-permute-start | bytes 2359304 | tf_op jit(solution)/shard_map/ppermute | solution.py:437
  375.5 48.2 %reduce-scatter.8.cloned.1.call-start = ((), (), s32[]{:S(2)}) async-start(), calls=%async_computation.7 | async-start | bytes 983040 | tf_op jit(solution)/shard_map/reduce_scatter | solution.py:440
  375.7 18.0 %collective-permute-start.11 = (bf16[4,48,2048]{2,1,0:T(8,128)(2,1)S(1)}, bf16[4,48,2048]{2,1,0:T(8,128)(2,1)S(1)}, u32[]{:S(2)}, u32[]{:S(2)}) collective-permute-start(bf16[4,48,2048]{2,1,0:T(8,128)(2,1)S(1)} %dynamic-slice_convert_fusion), channel_id=1, source_target_pairs={{0,16},{16,0},{1,17},{17,1},{2,18},{18,2},{3,19},{19,3},{4,20},{20... | collective-permute-start | bytes 2359304 | tf_op jit(solution)/shard_map/ppermute | solution.py:437
Sparse Core Ops, SparseCore 0:
  60.2 103.6 reduce-scatter.3
  165.7 26.6 all-gather.11
  194.8 35.5 all-gather.9
  244.0 18.4 all-gather.7
  375.6 23.1 reduce-scatter.5
  401.0 22.6 reduce-scatter.7
